TPU v7x, 32 devices: a whole 2x2x4 slice. The times are simulated.
32 devices in a mesh: dp: 4 (over y, core), tensor: 8 (over z, x).
Axes of the slice: x: 2, y: 2, z: 4, core: 2. Of those that a mesh axis runs over, the one named last changes fastest.
Arguments:
- grads: bfloat16 [4, 2, 7168, 2048], P('dp', None, 'tensor'), may hold values from -6 to 6
- master: float32 [2, 7168, 2048], P(None, 'dp', 'tensor'), may hold values from -0.0625 to 0.0625
- moment1: float32 [2, 7168, 2048], P(None, 'dp', 'tensor'), may hold values from -3 to 3
- moment2: float32 [2, 7168, 2048], P(None, 'dp', 'tensor'), may hold values from 1 to 30
- tokens: bfloat16 [1024, 7168], P('dp'), may hold values from -6 to 6
- route: int32 [512], P('dp'), may hold values from 0 to 255, as said below
Outputs:
- new_master: float32 [2, 7168, 2048], P(None, 'dp', 'tensor')
- new_moment1: float32 [2, 7168, 2048], P(None, 'dp', 'tensor')
- new_moment2: float32 [2, 7168, 2048], P(None, 'dp', 'tensor')
- rollout: bfloat16 [2, 7168, 2048], P(None, None, 'tensor')
- hidden: bfloat16 [512, 2048], P('dp', 'tensor')
Inputs may be any that keep to these rules, and one draw needn't show every extreme that they name: route[i] indexes one of the 256 tokens of the data rank that holds routed row i; within one data rank's 128 routed rows no token appears twice.
All inputs are finite; a program needn't handle non-finite values.
Results may differ from a plain program's by a relative error of at most 0.019.
Values may be sent and summed in bfloat16 or wider, within the bound.
No kernel may reach another device: no remote copies, remote signals or barrier semaphores. Data moves between devices by JAX's collectives and lax.ppermute only.
A program may use at most 128 MiB of HBM per device.

v0:
```python
import jax
import jax.numpy as jnp
from jax import lax
from jax.sharding import PartitionSpec as P


def body(grads, master, moment1, moment2, tokens, route):
    tensor_count = lax.axis_size("tensor")
    rank_count = lax.axis_size("dp")
    grad_local = grads[0]
    rows_tensor = grad_local.shape[1]
    hidden_width = grad_local.shape[2]
    col_width = hidden_width // tensor_count
    slab = rows_tensor // rank_count
    summed = lax.psum_scatter(grad_local, "dp", scatter_dimension=1, tiled=True).astype(jnp.float32)
    pieces = summed.reshape(2, slab, tensor_count, col_width)
    spread = lax.all_to_all(
        pieces.astype(jnp.bfloat16), "tensor", split_axis=2, concat_axis=1, tiled=True
    ).astype(pieces.dtype)
    spread = spread.reshape(2, rank_count, tensor_count // rank_count, slab, col_width)
    owned = lax.all_to_all(
        spread.astype(jnp.bfloat16), "dp", split_axis=1, concat_axis=3, tiled=True
    ).astype(spread.dtype)
    grad_total = owned.reshape(2, rows_tensor * tensor_count // rank_count, col_width)
    new_moment1 = 0.9 * moment1 + 0.1 * grad_total
    new_moment2 = 0.95 * moment2 + 0.05 * grad_total * grad_total
    first_fix = 1.0 - 0.9**10
    second_fix = 1.0 - 0.95**10
    step_size = (
        new_moment1 / first_fix / (jnp.sqrt(new_moment2 / second_fix) + 1e-08) + 0.1 * master
    )
    new_master = master - 0.003 * step_size
    rollout_shard = new_master.astype(jnp.bfloat16)
    replicated = lax.all_gather(rollout_shard, "dp", axis=1, tiled=True)
    picked = jnp.take(tokens, route, axis=0)
    both = jnp.einsum("rd,kdh->rkh", picked, replicated, preferred_element_type=jnp.float32)
    hidden = (jax.nn.silu(both[:, 0, :]) * both[:, 1, :]).astype(jnp.bfloat16)
    return (new_master, new_moment1, new_moment2, replicated, hidden)


def solution(mesh):
    in_specs = (
        P("dp", None, "tensor", None),
        P(None, "dp", "tensor"),
        P(None, "dp", "tensor"),
        P(None, "dp", "tensor"),
        P("dp", None),
        P("dp"),
    )
    out_specs = (
        P(None, "dp", "tensor"),
        P(None, "dp", "tensor"),
        P(None, "dp", "tensor"),
        P(None, None, "tensor"),
        P("dp", "tensor"),
    )
    return jax.shard_map(body, mesh=mesh, in_specs=in_specs, out_specs=out_specs, check_vma=False)
```

profile of v0, /device:TPU:0, one launch (start us, length us, event | category | flops | bytes accessed | tf_op | source)
XLA Modules:
  0.0 229.7 jit_solution(10080741824321627601)
XLA Ops:
  7.2 0.0 reduce-scatter.2.cloned.1.call-start
  7.2 0.7 reduce-scatter.2.cloned.1.call-update
  7.9 0.0 all-gather.2.cloned.1.call-start
  7.9 71.3 %reduce-scatter.2.cloned.1.call-done = bf16[2,224,2048]{2,1,0:T(8,128)(2,1)} async-done(((bf16[2,896,2048]{2,1,0:T(8,128)(2,1)}), bf16[2,224,2048]{2,1,0:T(8,128)(2,1)}) %reduce-scatter.2.cloned.1.call-update) | async-done | bytes 1835024 | tf_op jit(solution)/shard_map/reduce_scatter | solution.py:15
  79.2 1.7 copy.21
  80.9 47.8 %all_to_all.27 = bf16[2,224,8,256]{3,1,0,2:T(8,128)(2,1)S(1)} all-to-all(bf16[2,224,8,256]{3,1,0,2:T(8,128)(2,1)S(1)} %bitcast.31), channel_id=1, replica_groups=mesh['dp'=4,'tensor'=8] {'tensor'}, dimensions={2} | all-to-all | bytes 3670016 | tf_op jit(solution)/shard_map/all_to_all | solution.py:17
  128.7 0.1 copy.16
  128.8 25.3 %all_to_all.28 = bf16[2,4,2,224,256]{4,3,2,0,1:T(8,128)(2,1)S(1)} all-to-all(bf16[2,4,2,224,256]{4,3,2,0,1:T(8,128)(2,1)S(1)} %copy.16), channel_id=1, replica_groups=mesh['dp'=4,'tensor'=8] {'dp'}, dimensions={1} | all-to-all | bytes 3670016 | tf_op jit(solution)/shard_map/all_to_all | solution.py:21
  154.1 0.4 convert_bitcast_fusion
  154.5 0.0 copy-start.1
  154.5 0.0 copy-start.2
  154.5 0.4 copy.17
  154.9 1.2 copy-done.3
  156.1 1.2 copy-done.1
  157.4 1.0 copy-done.2
  158.4 5.7 %fusion.9 = (bf16[2,1792,256]{2,1,0:T(8,128)(2,1)}, f32[2,1792,256]{2,1,0:T(8,128)}, f32[2,1792,256]{2,1,0:T(8,128)}, f32[2,1792,256]{2,1,0:T(8,128)}) fusion(f32[2,1792,256]{2,1,0:T(8,128)S(1)} %copy-done.1, f32[2,1792,256]{2,1,0:T(8,128)S(1)} %bitcast.29, f32[2,1792,256]{2,1,0:T(8,128)S(1)} %copy-done.2, f32[2,1792,256]{2,1,0:T(8,128)S(1)} %copy-done.3), kind=kLoop, calls=%fused_computation.20 | loop fusion | flops 14680064 | bytes 27525120 | tf_op jit(solution)/shard_map/convert_element_type | solution.py:33
  164.1 0.0 all-gather.2.cloned.1.call-update
  164.1 0.0 copy-done.4
  164.1 5.9 %gather_fusion = bf16[128,7168]{1,0:T(8,128)(2,1)S(1)} fusion(bf16[256,7168]{1,0:T(8,128)(2,1)} %param.10, s32[1024]{0:T(1024)S(1)} %pad_clamp_fusion), kind=kCustom, calls=%fused_computation | custom fusion | bytes 3670528 | tf_op jit(solution)/shard_map/jit(_take)/gather | solution.py:35
  170.0 44.6 %all-gather.2.cloned.1.call-done = bf16[2,7168,256]{2,1,0:T(8,128)(2,1)} async-done(((bf16[2,1792,256]{2,1,0:T(8,128)(2,1)}), bf16[2,7168,256]{2,1,0:T(8,128)(2,1)}) %all-gather.2.cloned.1.call-update) | async-done | bytes 7340048 | tf_op jit(solution)/shard_map/all_gather | solution.py:34
  214.7 4.4 %fusion.1 = f32[128,2,256]{2,0,1:T(8,128)S(1)} fusion(bf16[2,7168,256]{2,1,0:T(8,128)(2,1)} %all-gather.2.cloned.1.call-done, bf16[128,7168]{1,0:T(8,128)(2,1)S(1)} %gather_fusion, pred[128]{0:T(512)(128)(4,1)S(1)} %compare_and_fusion), kind=kOutput, calls=%fused_computation.7 | convolution fusion | flops 940441600 | bytes 9437312 | tf_op jit(solution)/shard_map/rd,kdh->rkh/dot_general | solution.py:36
  219.0 0.7 fusion.7
  219.7 0.1 copy-done
  219.8 3.0 %copy.23 = bf16[2,7168,256]{2,1,0:T(8,128)(2,1)} copy(bf16[2,7168,256]{2,1,0:T(8,128)(2,1)S(1)} %copy-done) | data formatting | bytes 14680064
  (6 shorter events, 0.0 us)
Async XLA Ops:
  7.2 72.0 %reduce-scatter.2.cloned.1.call-start = ((), (), s32[]{:S(2)}) async-start(), calls=%async_computation.3 | async-start | bytes 9175040 | tf_op jit(solution)/shard_map/reduce_scatter | solution.py:15
  7.9 206.7 %all-gather.2.cloned.1.call-start = ((), (), s32[]{:S(2)}) async-start(), calls=%async_computation.4 | async-start | bytes 9175040 | tf_op jit(solution)/shard_map/all_gather | solution.py:34
  154.1 2.0 copy-start.3
  154.5 2.9 %copy-start.1 = (f32[2,1792,256]{2,1,0:T(8,128)S(1)}, f32[2,1792,256]{2,1,0:T(8,128)}, u32[]{:S(2)}) copy-start(f32[2,1792,256]{2,1,0:T(8,128)} %param.7) | copy-start | bytes 11010052
  154.5 3.9 %copy-start.2 = (f32[2,1792,256]{2,1,0:T(8,128)S(1)}, f32[2,1792,256]{2,1,0:T(8,128)}, u32[]{:S(2)}) copy-start(f32[2,1792,256]{2,1,0:T(8,128)} %param.8) | copy-start | bytes 11010052
  158.4 5.7 %copy-start.4 = (s32[128]{0:T(128)S(1)}, s32[128]{0:T(128)}, u32[]{:S(2)}) copy-start(s32[128]{0:T(128)} %param.11) | copy-start | bytes 1540
  214.6 5.2 %copy-start = (bf16[2,7168,256]{2,1,0:T(8,128)(2,1)S(1)}, bf16[2,7168,256]{2,1,0:T(8,128)(2,1)}, u32[]{:S(2)}) copy-start(bf16[2,7168,256]{2,1,0:T(8,128)(2,1)} %all-gather.2.cloned.1.call-done) | copy-start | bytes 22020100
Sparse Core Ops, SparseCore 0:
  10.5 68.6 reduce-scatter.1
  164.2 50.3 all-gather.1
where the time goes:
time: 230 us
  waiting for transfers between devices  117 us (51%)
  blocking collectives  73.1 us (32%)
  local copies, waits for them, and re-layouts  14.7 us (6%)
  between operations  14.1 us (6%)
  other arithmetic  6.75 us (3%)
  matrix products  4.38 us (2%)
    reduce_scatter x1, waiting for transfers between devices, body(): lax.psum_scatter(grad_local, 'dp', scatter_dimension=1, tiled=True)  71.3 us
    all_to_all x1, blocking collectives, body(): lax.all_to_all(pieces.astype(jnp.bfloat16), 'tensor', split_axis=2, conca...  47.8 us
    all_gather x1, waiting for transfers between devices, body(): replicated = lax.all_gather(rollout_shard, 'dp', axis=1, tiled=True)  44.6 us
    all_to_all x1, blocking collectives, body(): lax.all_to_all(spread.astype(jnp.bfloat16), 'dp', split_axis=1, concat_ax...  25.3 us
    unnamed x11, local copies, waits for them, and re-layouts  6.67 us
    gather x1, local copies, waits for them, and re-layouts, body(): picked = jnp.take(tokens, route, axis=0)  5.88 us
    convert_element_type x1, other arithmetic, body(): rollout_shard = new_master.astype(jnp.bfloat16)  5.66 us
  transfers between devices with their start and end apart: 2, of which 2 were waited for; matrix products, arithmetic and copies ran while one was open for 3% of the time, Pallas kernels for 0%

commit v1 on v0

--- a/solution.py
+++ b/solution.py
@@ -31,7 +31,12 @@
     )
     new_master = master - 0.003 * step_size
     rollout_shard = new_master.astype(jnp.bfloat16)
-    replicated = lax.all_gather(rollout_shard, "dp", axis=1, tiled=True)
+    ring = [rollout_shard]
+    for hop in range(3):
+        ring.append(lax.ppermute(ring[-1], "dp", [(dev, (dev + 1) % 4) for dev in range(4)]))
+    replicated = jnp.roll(
+        jnp.concatenate(ring[::-1], axis=1), (lax.axis_index("dp") + 1) * ring[0].shape[1], axis=1
+    )
     picked = jnp.take(tokens, route, axis=0)
     both = jnp.einsum("rd,kdh->rkh", picked, replicated, preferred_element_type=jnp.float32)
     hidden = (jax.nn.silu(both[:, 0, :]) * both[:, 1, :]).astype(jnp.bfloat16)

time: 230 us -> 266 us (1.16)
  local copies, waits for them, and re-layouts: 14.7 us -> 37.9 us
  waiting for transfers between devices: 117 us -> 133 us
  matrix products: 4.38 us -> 1.16 us
    ppermute x0 -> x3, waiting for transfers between devices: none -> 61.2 us  [body(): lax.ppermute(ring[-1], 'dp', [(dev, (dev + 1) % 4) for dev in range(4)])]
    all_gather x1 -> x0, waiting for transfers between devices: 44.6 us -> none  [body(): replicated = lax.all_gather(rollout_shard, 'dp', axis=1, tiled=True)]
    unnamed x11 -> x23, local copies, waits for them, and re-layouts: 6.67 us -> 22.2 us
    dynamic_slice x0 -> x1, local copies, waits for them, and re-layouts: none -> 4.98 us  [body(): jnp.roll(jnp.concatenate(ring[::-1], axis=1), (lax.axis_index('dp') + 1)...]
    dot_general x1, matrix products: 4.38 us -> 1.16 us  [body(): jnp.einsum('rd,kdh->rkh', picked, replicated, preferred_element_type=jnp....]
  transfers between devices with their start and end apart: 2 -> 4, of which waited for: 2 -> 4; matrix products, arithmetic and copies ran while one was open for 3% -> 3% of each run, Pallas kernels for 0% -> 0%
where the time goes in v1:
time: 266 us
  waiting for transfers between devices  133 us (50%)
  blocking collectives  73.1 us (27%)
  local copies, waits for them, and re-layouts  37.9 us (14%)
  between operations  14.1 us (5%)
  other arithmetic  6.16 us (2%)
    reduce_scatter x1, waiting for transfers between devices, body(): lax.psum_scatter(grad_local, 'dp', scatter_dimension=1, tiled=True)  71.3 us
    ppermute x3, waiting for transfers between devices, body(): lax.ppermute(ring[-1], 'dp', [(dev, (dev + 1) % 4) for dev in range(4)])  61.2 us
    all_to_all x1, blocking collectives, body(): lax.all_to_all(pieces.astype(jnp.bfloat16), 'tensor', split_axis=2, conca...  47.8 us
    all_to_all x1, blocking collectives, body(): lax.all_to_all(spread.astype(jnp.bfloat16), 'dp', split_axis=1, concat_ax...  25.3 us
    unnamed x23, local copies, waits for them, and re-layouts  22.2 us
    gather x1, local copies, waits for them, and re-layouts, body(): picked = jnp.take(tokens, route, axis=0)  7.15 us
  transfers between devices with their start and end apart: 4, of which 4 were waited for; matrix products, arithmetic and copies ran while one was open for 3% of the time, Pallas kernels for 0%

profile of v1, /device:TPU:0, one launch (start us, length us, event | category | flops | bytes accessed | tf_op | source)
XLA Modules:
  0.0 265.6 jit_solution(1653928580319128521)
XLA Ops:
  7.9 71.3 %reduce-scatter.2.cloned.1.call-done = bf16[2,224,2048]{2,1,0:T(8,128)(2,1)} async-done(((bf16[2,896,2048]{2,1,0:T(8,128)(2,1)}), bf16[2,224,2048]{2,1,0:T(8,128)(2,1)}) %reduce-scatter.2.cloned.1.call-update) | async-done | bytes 1835024 | tf_op jit(solution)/shard_map/reduce_scatter | solution.py:15
  79.2 1.7 copy.21
  80.9 47.8 %all_to_all.27 = bf16[2,224,8,256]{3,1,0,2:T(8,128)(2,1)S(1)} all-to-all(bf16[2,224,8,256]{3,1,0,2:T(8,128)(2,1)S(1)} %bitcast.31), channel_id=1, replica_groups=mesh['dp'=4,'tensor'=8] {'tensor'}, dimensions={2} | all-to-all | bytes 3670016 | tf_op jit(solution)/shard_map/all_to_all | solution.py:17
  128.8 25.3 %all_to_all.28 = bf16[2,4,2,224,256]{4,3,2,0,1:T(8,128)(2,1)S(1)} all-to-all(bf16[2,4,2,224,256]{4,3,2,0,1:T(8,128)(2,1)S(1)} %copy.16), channel_id=1, replica_groups=mesh['dp'=4,'tensor'=8] {'dp'}, dimensions={1} | all-to-all | bytes 3670016 | tf_op jit(solution)/shard_map/all_to_all | solution.py:21
  154.9 1.2 copy-done.5
  156.1 1.2 copy-done.3
  157.4 1.0 copy-done.4
  158.4 5.1 %fusion.9 = (bf16[2,1792,256]{2,1,0:T(8,128)(2,1)S(1)}, f32[2,1792,256]{2,1,0:T(8,128)}, f32[2,1792,256]{2,1,0:T(8,128)}, f32[2,1792,256]{2,1,0:T(8,128)}) fusion(f32[2,1792,256]{2,1,0:T(8,128)S(1)} %copy-done.3, f32[2,1792,256]{2,1,0:T(8,128)S(1)} %bitcast.29, f32[2,1792,256]{2,1,0:T(8,128)S(1)} %copy-done.4, f32[2,1792,256]{2,1,0:T(8,128)S(1)} %copy-done.5), kind=kLoop, calls=%fused_computation.29 | loop fusion | flops 14680064 | bytes 27525120 | tf_op jit(solution)/shard_map/convert_element_type | solution.py:33
  163.5 22.6 %collective-permute-done = bf16[2,1792,256]{2,1,0:T(8,128)(2,1)S(1)} collective-permute-done((bf16[2,1792,256]{2,1,0:T(8,128)(2,1)S(1)}, bf16[2,1792,256]{2,1,0:T(8,128)(2,1)S(1)}, u32[]{:S(2)}, u32[]{:S(2)}) %collective-permute-start) | collective-permute-done | bytes 1835040 | tf_op jit(solution)/shard_map/ppermute | solution.py:36
  186.1 1.2 copy-done.1
  187.4 22.8 %collective-permute-done.1 = bf16[2,1792,256]{2,1,0:T(8,128)(2,1)} collective-permute-done((bf16[2,1792,256]{2,1,0:T(8,128)(2,1)S(1)}, bf16[2,1792,256]{2,1,0:T(8,128)(2,1)}, u32[]{:S(2)}, u32[]{:S(2)}) %collective-permute-start.1) | collective-permute-done | bytes 1835040 | tf_op jit(solution)/shard_map/ppermute | solution.py:36
  210.2 7.1 %gather_fusion = bf16[128,7168]{1,0:T(8,128)(2,1)} fusion(bf16[256,7168]{1,0:T(8,128)(2,1)} %param.10, s32[1024]{0:T(1024)S(1)} %pad_clamp_fusion), kind=kCustom, calls=%fused_computation | custom fusion | bytes 3670528 | tf_op jit(solution)/shard_map/jit(_take)/gather | solution.py:40
  217.3 15.8 %collective-permute-done.2 = bf16[2,1792,256]{2,1,0:T(8,128)(2,1)} collective-permute-done((bf16[2,1792,256]{2,1,0:T(8,128)(2,1)}, bf16[2,1792,256]{2,1,0:T(8,128)(2,1)}, u32[]{:S(2)}, u32[]{:S(2)}) %collective-permute-start.2) | collective-permute-done | bytes 1835040 | tf_op jit(solution)/shard_map/ppermute | solution.py:36
  233.1 2.9 %constant_dynamic-update-slice_fusion.7 = bf16[2,14336,256]{2,1,0:T(8,128)(2,1)} fusion(bf16[2,1792,256]{2,1,0:T(8,128)(2,1)} %collective-permute-done.2), kind=kLoop, calls=%fused_computation.23 | loop fusion | bytes 3670016
  236.0 2.9 %constant_dynamic-update-slice_fusion.6 = bf16[2,14336,256]{2,1,0:T(8,128)(2,1)} fusion(bf16[2,14336,256]{2,1,0:T(8,128)(2,1)} %constant_dynamic-update-slice_fusion.7, bf16[2,1792,256]{2,1,0:T(8,128)(2,1)} %collective-permute-done.1), kind=kLoop, calls=%fused_computation.22 | loop fusion | bytes 3670016
  238.9 1.3 constant_dynamic-update-slice_fusion.5
  240.2 1.4 constant_dynamic-update-slice_fusion.4
  241.6 2.8 %constant_dynamic-update-slice_fusion.3 = bf16[2,14336,256]{2,1,0:T(8,128)(2,1)} fusion(bf16[2,14336,256]{2,1,0:T(8,128)(2,1)} %constant_dynamic-update-slice_fusion.4, bf16[2,1792,256]{2,1,0:T(8,128)(2,1)} %collective-permute-done.2), kind=kLoop, calls=%fused_computation.19 | loop fusion | bytes 3670016
  244.4 2.9 %constant_dynamic-update-slice_fusion.2 = bf16[2,14336,256]{2,1,0:T(8,128)(2,1)} fusion(bf16[2,14336,256]{2,1,0:T(8,128)(2,1)} %constant_dynamic-update-slice_fusion.3, bf16[2,1792,256]{2,1,0:T(8,128)(2,1)} %collective-permute-done.1), kind=kLoop, calls=%fused_computation.18 | loop fusion | bytes 3670016
  247.3 1.4 constant_dynamic-update-slice_fusion.1
  248.7 1.4 constant_dynamic-update-slice_fusion
  250.1 5.0 %constant_dynamic-slice_fusion = bf16[2,7168,256]{2,1,0:T(8,128)(2,1)S(1)} fusion(bf16[2,14336,256]{2,1,0:T(8,128)(2,1)} %constant_dynamic-update-slice_fusion, s32[]{:T(128)S(6)} %select_n.23), kind=kLoop, calls=%fused_computation.27 | loop fusion | bytes 14680068 | tf_op jit(solution)/shard_map/jit(_roll_dynamic)/dynamic_slice | solution.py:37
  255.1 1.2 fusion.1
  256.2 1.9 copy-done
  (23 shorter events, 2.3 us)
Async XLA Ops:
  7.2 72.0 %reduce-scatter.2.cloned.1.call-start = ((), (), s32[]{:S(2)}) async-start(), calls=%async_computation.3 | async-start | bytes 9175040 | tf_op jit(solution)/shard_map/reduce_scatter | solution.py:15
  154.1 2.0 copy-start.5
  154.5 2.9 %copy-start.3 = (f32[2,1792,256]{2,1,0:T(8,128)S(1)}, f32[2,1792,256]{2,1,0:T(8,128)}, u32[]{:S(2)}) copy-start(f32[2,1792,256]{2,1,0:T(8,128)} %param.7) | copy-start | bytes 11010052
  154.5 3.9 %copy-start.4 = (f32[2,1792,256]{2,1,0:T(8,128)S(1)}, f32[2,1792,256]{2,1,0:T(8,128)}, u32[]{:S(2)}) copy-start(f32[2,1792,256]{2,1,0:T(8,128)} %param.8) | copy-start | bytes 11010052
  158.4 51.7 %copy-start.7 = (s32[128]{0:T(128)S(1)}, s32[128]{0:T(128)}, u32[]{:S(2)}) copy-start(s32[128]{0:T(128)} %param.11) | copy-start | bytes 1540
  163.5 22.7 %collective-permute-start = (bf16[2,1792,256]{2,1,0:T(8,128)(2,1)S(1)}, bf16[2,1792,256]{2,1,0:T(8,128)(2,1)S(1)}, u32[]{:S(2)}, u32[]{:S(2)}) collective-permute-start(bf16[2,1792,256]{2,1,0:T(8,128)(2,1)S(1)} %get-tuple-element.5), channel_id=1, source_target_pairs={{0,8},{8,16},{16,24},{24,0},{1,9},{9,17},{17,25},{25,1},{2,10},{10... | collective-permute-start | bytes 5505032 | tf_op jit(solution)/shard_map/ppermute | solution.py:36
  186.1 1.2 copy-start.1
  187.4 22.8 %collective-permute-start.1 = (bf16[2,1792,256]{2,1,0:T(8,128)(2,1)S(1)}, bf16[2,1792,256]{2,1,0:T(8,128)(2,1)}, u32[]{:S(2)}, u32[]{:S(2)}) collective-permute-start(bf16[2,1792,256]{2,1,0:T(8,128)(2,1)S(1)} %collective-permute-done), channel_id=1, source_target_pairs={{0,8},{8,16},{16,24},{24,0},{1,9},{9,17},{17,25},{25,1},{2,10},{10... | collective-permute-start | bytes 5505032 | tf_op jit(solution)/shard_map/ppermute | solution.py:36
  210.1 23.0 %collective-permute-start.2 = (bf16[2,1792,256]{2,1,0:T(8,128)(2,1)}, bf16[2,1792,256]{2,1,0:T(8,128)(2,1)}, u32[]{:S(2)}, u32[]{:S(2)}) collective-permute-start(bf16[2,1792,256]{2,1,0:T(8,128)(2,1)} %collective-permute-done.1), channel_id=1, source_target_pairs={{0,8},{8,16},{16,24},{24,0},{1,9},{9,17},{17,25},{25,1},{2,10},{10... | collective-permute-start | bytes 5505032 | tf_op jit(solution)/shard_map/ppermute | solution.py:36
  217.3 21.6 %copy-start.2 = (bf16[2,1792,256]{2,1,0:T(8,128)(2,1)S(1)}, bf16[2,1792,256]{2,1,0:T(8,128)(2,1)}, u32[]{:S(2)}) copy-start(bf16[2,1792,256]{2,1,0:T(8,128)(2,1)} %copy-done.1) | copy-start | bytes 5505028
  250.1 5.0 %copy-start.6 = (bf16[128,7168]{1,0:T(8,128)(2,1)S(1)}, bf16[128,7168]{1,0:T(8,128)(2,1)}, u32[]{:S(2)}) copy-start(bf16[128,7168]{1,0:T(8,128)(2,1)} %gather_fusion) | copy-start | bytes 5505028
  255.1 3.1 %copy-start = (bf16[2,7168,256]{2,1,0:T(8,128)(2,1)}, bf16[2,7168,256]{2,1,0:T(8,128)(2,1)S(1)}, u32[]{:S(2)}) copy-start(bf16[2,7168,256]{2,1,0:T(8,128)(2,1)S(1)} %constant_dynamic-slice_fusion) | copy-start | bytes 22020100
Sparse Core Ops, SparseCore 0:
  10.5 68.6 reduce-scatter.1
